TPU v7x, 512 devices: a whole 4x8x8 slice. The times are simulated.
512 devices in a mesh: section: 4 (over z_hi), row: 4 (over z_lo, core), col: 32 (over y, x).
Axes of the slice: x: 4, y: 8, z: 8 (z_hi: 4, z_lo: 2; z = z_hi * 2 + z_lo), core: 2. Of those that a mesh axis runs over, the one named last changes fastest.
Arguments:
- state: bfloat16 [4, 128, 1024, 256], P('section', 'row', 'col'), may hold values from -6 to 6
- fresh: bfloat16 [128, 1024, 256], P('row', 'col'), may hold values from -6 to 6
- conv_first: bfloat16 [4, 3, 3, 256, 256], P('section'), may hold values from -0.125 to 0.125
- conv_second: bfloat16 [4, 3, 3, 256, 256], P('section'), may hold values from -0.125 to 0.125
- gains: float32 [4, 2, 256], P('section'), may hold values from 0.1 to 1.9
- shifts: float32 [4, 2, 256], P('section'), may hold values from -2.4 to 2.4
Outputs:
- blocks: bfloat16 [2, 4, 128, 1024, 256], P(None, 'section', 'row', 'col')
All inputs are finite; a program needn't handle non-finite values.
Results may differ from a plain program's by a relative error of at most 0.005.
Values may be sent and summed in bfloat16 or wider, within the bound.
No kernel may reach another device: no remote copies, remote signals or barrier semaphores. Data moves between devices by JAX's collectives and lax.ppermute only.
A program may use at most 64 MiB of HBM per device.

v0:
```python
import functools

import jax
import jax.numpy as jnp
from jax import lax
from jax.experimental import pallas as pl
from jax.experimental.pallas import tpu as pltpu
from jax.sharding import PartitionSpec as P


BF16 = jnp.bfloat16
F32 = jnp.float32
VMEM_LIMIT = 24 * 1024 * 1024
SIDE = 16
MOST = 19


def largest_divisor(n, most):
    return next(d for d in range(most, 0, -1) if n % d == 0)


def dots(source, spot, size, pitch, weights):
    chan = weights.shape[1]
    acc = None
    for tap in range(3):
        part = jnp.dot(
            source[pl.ds(pl.multiple_of(spot + tap * pitch, 8), size * pitch), :],
            weights[pl.ds(tap * 3 * chan, 3 * chan), :],
            preferred_element_type=F32,
        )
        acc = part if acc is None else acc + part
    return acc


def stack_row(x3, at, row):
    pitch, chan = row.shape
    spot = pl.ds(pl.multiple_of(at * pitch, 8), pitch)
    x3[spot, 0:chan] = pltpu.roll(row, 1, 0).astype(BF16)
    x3[spot, chan : 2 * chan] = row.astype(BF16)
    x3[spot, 2 * chan :] = pltpu.roll(row, pitch - 1, 0).astype(BF16)


def kept(flags, extent, row_id, col_keep):
    inside = ((row_id >= 0) | (flags[0] == 0)) & ((row_id < extent) | (flags[1] == 0))
    return col_keep & inside


def wide_keep(flags, pitch, reach):
    j = lax.broadcasted_iota(jnp.int32, (pitch, 1), 0)
    low, high = j < reach, j >= pitch - reach
    return jnp.logical_not(low & (flags[2] == 1)) & jnp.logical_not(high & (flags[3] == 1))


def convolutions(flags, extent, pitch, reach, first, count, x3, h3, weights, emit):
    gains, shifts, k1, k2 = weights
    chan = k1.shape[1]
    col_keep = wide_keep(flags, pitch, reach)
    gain1, shift1 = gains[0:1], shifts[0:1]
    gain2, shift2 = gains[1:2], shifts[1:2]
    size1 = largest_divisor(count + 2, MOST)

    def hidden_block(b):
        spot = b * (size1 * pitch)
        acc = jnp.maximum(gain1 * dots(x3, spot, size1, pitch, k1) + shift1, 0.0)
        for r in range(size1):
            keep = kept(flags, extent, first - 1 + b * size1 + r, col_keep)
            stack_row(h3, b * size1 + r, jnp.where(keep, acc[r * pitch : (r + 1) * pitch], 0.0))

    pl.loop(0, (count + 2) // size1)(hidden_block)
    size2 = largest_divisor(count, MOST)
    for b in range(count // size2):
        i = b * size2
        acc = gain2 * dots(h3, i * pitch, size2, pitch, k2) + shift2
        base = x3[pl.ds((i + 2) * pitch, size2 * pitch), chan : 2 * chan].astype(F32)
        acc = jnp.maximum(base + acc, 0.0)
        values = []
        for r in range(size2):
            keep = kept(flags, extent, first + i + r, col_keep)
            values.append(jnp.where(keep, acc[r * pitch : (r + 1) * pitch], 0.0))
        emit(i, values)


def run_copies(pairs, sems):
    copies = [pltpu.make_async_copy(a, b, sems.at[n]) for n, (a, b) in enumerate(pairs)]
    for copy in copies:
        copy.start()
    for copy in copies:
        copy.wait()


def edge_kernel(x, fresh, down, up, sems):
    rows = x.shape[0]
    run_copies(
        (
            (x.at[pl.ds(rows - 4, 4)], down.at[pl.ds(0, 4)]),
            (fresh.at[pl.ds(rows - 2, 2)], down.at[pl.ds(4, 2)]),
            (x.at[pl.ds(0, 4)], up.at[pl.ds(0, 4)]),
            (fresh.at[pl.ds(0, 2)], up.at[pl.ds(4, 2)]),
        ),
        sems,
    )


def load_kernel(*refs):
    half = (len(refs) - 1) // 2
    fresh, sources, targets = refs[0], refs[1:half], refs[half:-1]
    cols = fresh.shape[1]
    sides = ((fresh.at[:, pl.ds(at, 8)], targets[n]) for n, at in enumerate((0, cols - 8)))
    run_copies((*sides, *zip(sources, targets[2:])), refs[-1])


def pack_kernel(x, fresh_low, fresh_high, top, bot, to_right, to_left, packed):
    rows, cols, _ = x.shape
    wide = 4 * (rows + 8)
    for side, out in ((1, to_right), (0, to_left)):
        edge = pl.ds((cols - 8) * side, 8)
        for n, (halo, keep) in enumerate(((4, 4), (2, 2))):
            for p in range(rows + 2 * halo):
                at = p - halo
                if at < 0:
                    piece = top[4 * n + p, edge]
                elif at >= rows:
                    piece = bot[4 * n + at - rows, edge]
                else:
                    piece = (fresh_low, fresh_high)[side][at] if n else x[at, edge]
                piece = piece.astype(F32)
                piece = piece[8 - keep :] if side else piece[:keep]
                spot = wide * n + keep * p
                packed[spot : spot + keep] = piece
        out[...] = packed[...].astype(BF16)


def extended_row(x, top, bot, at, halo, skip):
    rows = x.shape[0]
    if at < 0:
        return top[skip + halo + at].astype(F32)
    if at >= rows:
        return bot[skip + at - rows].astype(F32)
    return x[at].astype(F32)


def main_kernel(flags, x, top, bot, gains, shifts, k1, k2, msg, x3, h3, inner):
    rows, cols, _ = x.shape
    keep = cols - 4
    for p in range(rows + 8):
        stack_row(x3, p, extended_row(x, top, bot, p - 4, 4, 0))

    def emit(i, values):
        for r, value in enumerate(values):
            inner[(i + r) * keep : (i + r + 1) * keep] = value[2 : cols - 2]

    weights = gains, shifts, k1, k2
    convolutions(flags, rows, cols, 0, -2, rows + 4, x3, h3, weights, emit)
    msg[...] = inner[...].astype(BF16)


def side_kernel(flags, x, top, bot, left, right, gains, shifts, k1, k2, msg, x3, h3, es, row):
    rows, cols, _ = x.shape
    for p in range(rows + 8):
        main = extended_row(x, top, bot, p - 4, 4, 0)
        row[p, 0:4] = left[4 * p : 4 * p + 4].astype(F32)
        row[p, 4:8] = main[0:4]
        row[p, 8:12] = main[cols - 4 : cols]
        row[p, 12:16] = right[4 * p : 4 * p + 4].astype(F32)
        stack_row(x3, p, row[p])

    def emit(i, values):
        for r, value in enumerate(values):
            n = i + r
            es[8 * n : 8 * n + 4] = value[2:6]
            es[8 * n + 4 : 8 * n + 8] = value[10:14]

    weights = gains, shifts, k1, k2
    convolutions(flags, rows, SIDE, 4, -2, rows + 4, x3, h3, weights, emit)
    msg[...] = es[...].astype(BF16)


def keep_kernel(main, sides, blocks, osc, row, sem, *, rows, cols):
    inner = cols - 4
    for n in range(rows):
        p = n + 2
        edge = sides[8 * p : 8 * p + 8].astype(F32)
        row[n, 0:2] = edge[2:4]
        row[n, 2 : cols - 2] = main[inner * p : inner * (p + 1)].astype(F32)
        row[n, cols - 2 : cols] = edge[4:6]
        osc[n * cols : (n + 1) * cols] = row[n].astype(BF16)
    copy = pltpu.make_async_copy(osc, blocks.at[pl.ds(0, rows * cols)], sem)
    copy.start()
    copy.wait()


def late_main_kernel(flags, main, fresh, top, bot, gains, shifts, k1, k2, out, x3, h3, row):
    rows, cols, chan = fresh.shape
    inner = cols - 4

    @pl.when(flags[4] == 1)
    def _():
        for p in range(rows + 4):
            row[p] = extended_row(fresh, top, bot, p - 2, 2, 4)

    @pl.when(flags[4] == 0)
    def _():
        for p in range(rows + 4):
            row[p, 0:2] = jnp.zeros((2, chan), F32)
            row[p, 2 : cols - 2] = main[inner * p : inner * (p + 1)].astype(F32)
            row[p, cols - 2 : cols] = jnp.zeros((2, chan), F32)

    for p in range(rows + 4):
        stack_row(x3, p, row[p])

    def emit(i, values):
        for r, value in enumerate(values):
            out[(i + r) * cols : (i + r + 1) * cols] = value.astype(BF16)

    weights = gains, shifts, k1, k2
    convolutions(flags, rows, cols, 0, 0, rows, x3, h3, weights, emit)


def late_side_kernel(
    flags, main, sides, middle, fresh, top, bot, left, right, gains, shifts, k1, k2, _, blocks, x3, h3, row,
    full, osc, sems
):
    rows, cols, _ = fresh.shape
    inner = cols - 4
    wide = 4 * (rows + 8)

    @pl.when(flags[4] == 1)
    def _():
        for p in range(rows + 4):
            own = extended_row(fresh, top, bot, p - 2, 2, 4)
            spot = wide + 2 * p
            row[p, 0:2] = left[spot : spot + 2].astype(F32)
            row[p, 2:8] = own[0:6]
            row[p, 8:14] = own[cols - 6 : cols]
            row[p, 14:16] = right[spot : spot + 2].astype(F32)

    @pl.when(flags[4] == 0)
    def _():
        for p in range(rows + 4):
            edge = sides[8 * p : 8 * p + 8].astype(F32)
            row[p, 0:4] = edge[0:4]
            row[p, 4:8] = main[inner * p : inner * p + 4].astype(F32)
            row[p, 8:12] = main[inner * (p + 1) - 4 : inner * (p + 1)].astype(F32)
            row[p, 12:16] = edge[4:8]

    for p in range(rows + 4):
        stack_row(x3, p, row[p])
    copies = []

    def emit(i, values):
        for r, value in enumerate(values):
            n = i + r
            here = slice(n * cols, (n + 1) * cols)
            full[n] = middle[here].astype(F32)
            full[n, 0:4] = value[2:6]
            full[n, cols - 4 : cols] = value[10:14]
            osc[here] = full[n].astype(BF16)
        size = len(values) * cols
        copy = pltpu.make_async_copy(
            osc.at[pl.ds(i * cols, size)],
            blocks.at[pl.ds((rows + i) * cols, size)],
            sems.at[len(copies)],
        )
        copy.start()
        copies.append(copy)

    weights = gains, shifts, k1, k2
    convolutions(flags, rows, SIDE, 2, 0, rows, x3, h3, weights, emit)
    for copy in copies:
        copy.wait()


SMEM = pl.BlockSpec(memory_space=pltpu.SMEM)
VM = pl.BlockSpec(memory_space=pltpu.VMEM)
ANY = pl.BlockSpec(memory_space=pl.ANY)
HBM = pl.BlockSpec(memory_space=pltpu.HBM)
PARAMS = dict(vmem_limit_bytes=VMEM_LIMIT)


def cost(count, pitch, chan):
    return pl.CostEstimate(
        flops=4 * 9 * count * pitch * chan * chan, bytes_accessed=3 * 1024 * 1024, transcendentals=0
    )


def tick_call(body, operands, out_shape, count, pitch, scratch, last=False):
    chan = out_shape[1]
    stacks = [
        pltpu.VMEM(((count + 4) * pitch, 3 * chan), BF16),
        pltpu.VMEM(((count + 2) * pitch, 3 * chan), BF16),
    ]
    spaces = [SMEM] + [VM] * (len(operands) - 1)
    if last:
        spaces[-1] = HBM
    return pl.pallas_call(
        body,
        out_shape=jax.ShapeDtypeStruct(out_shape, BF16),
        in_specs=spaces,
        out_specs=HBM if last else VM,
        scratch_shapes=stacks + scratch,
        input_output_aliases={len(operands) - 1: 0} if last else {},
        compiler_params=pltpu.CompilerParams(**PARAMS),
        cost_estimate=cost(count, pitch, chan),
    )(*operands)


def edge_call(x, fresh):
    shape = jax.ShapeDtypeStruct((6,) + x.shape[1:], BF16)
    return pl.pallas_call(
        edge_kernel,
        out_shape=[shape, shape],
        in_specs=[HBM, HBM],
        out_specs=[VM, VM],
        scratch_shapes=[pltpu.SemaphoreType.DMA((4,))],
        compiler_params=pltpu.CompilerParams(**PARAMS),
        name="edge",
    )(x, fresh)


def load_call(fresh, values):
    rows, _, chan = fresh.shape
    shapes = [(rows, 8, chan)] * 2 + [v.shape for v in values]
    kinds = [BF16] * 2 + [v.dtype for v in values]
    return pl.pallas_call(
        load_kernel,
        out_shape=[jax.ShapeDtypeStruct(shape, kind) for shape, kind in zip(shapes, kinds)],
        in_specs=[HBM] * (len(values) + 1),
        out_specs=[VM] * len(shapes),
        scratch_shapes=[pltpu.SemaphoreType.DMA((len(shapes),))],
        compiler_params=pltpu.CompilerParams(**PARAMS),
        cost_estimate=pl.CostEstimate(flops=1 << 30, bytes_accessed=4 << 20, transcendentals=0),
        name="load",
    )(fresh, *values)


def pack_call(x, sides, top, bot):
    rows, _, chan = x.shape
    total = 4 * (rows + 8) + 2 * (rows + 4)
    return pl.pallas_call(
        pack_kernel,
        out_shape=[jax.ShapeDtypeStruct((total, chan), BF16)] * 2,
        in_specs=[VM] * 5,
        out_specs=[VM, VM],
        scratch_shapes=[pltpu.VMEM((total, chan), F32)],
        compiler_params=pltpu.CompilerParams(**PARAMS),
        name="pack",
    )(x, *sides, top, bot)


def keep_call(main, sides, shape):
    rows, cols, chan = shape
    return pl.pallas_call(
        functools.partial(keep_kernel, rows=rows, cols=cols),
        out_shape=jax.ShapeDtypeStruct((2 * rows * cols, chan), BF16),
        in_specs=[VM, VM],
        out_specs=HBM,
        scratch_shapes=[
            pltpu.VMEM((rows * cols, chan), BF16),
            pltpu.VMEM((rows, cols, chan), F32),
            pltpu.SemaphoreType.DMA,
        ],
        compiler_params=pltpu.CompilerParams(**PARAMS),
        name="keep",
    )(main, sides)


def moves(axis, by):
    size = lax.axis_size(axis)
    return [(i, i + by) for i in range(size) if 0 <= i + by < size]


def tied(value, after):
    return lax.optimization_barrier((value, after))[0]


def in_hbm(value):
    return pltpu.with_memory_space_constraint(value, pltpu.HBM)


def per_device(state, fresh, conv_first, conv_second, gains, shifts):
    x = state[0]
    rows, cols, chan = x.shape
    flat = (9 * chan, chan)
    values = (fresh, x, gains[0], shifts[0], conv_first[0].reshape(flat), conv_second[0].reshape(flat))
    values = [in_hbm(v) for v in values]
    row, col = lax.axis_index("row"), lax.axis_index("col")
    flags = jnp.stack(
        [
            row == 0,
            row == lax.axis_size("row") - 1,
            col == 0,
            col == lax.axis_size("col") - 1,
            lax.axis_index("section") == 0,
        ]
    ).astype(jnp.int32)
    down, up = edge_call(values[1], values[0])
    bot = lax.ppermute(up, "row", moves("row", -1))
    top = lax.ppermute(down, "row", moves("row", 1))
    *sides, x, gain, shift, k1, k2 = load_call(values[0], values[1:])
    params = gain, shift, k1, k2
    tall = rows + 4

    def rows_of(*shape):
        return pltpu.VMEM((*shape, chan), F32)

    inner = tall * (cols - 4)
    operands = (flags, x, top, bot, *params)
    main = tick_call(main_kernel, operands, (inner, chan), tall, cols, [rows_of(inner)])

    def onward(message):
        return lax.ppermute(message, "section", moves("section", 1))

    got_main = onward(main)
    to_right, to_left = pack_call(x, sides, tied(top, main), bot)
    left = lax.ppermute(to_right, "col", moves("col", 1))
    right = lax.ppermute(to_left, "col", moves("col", -1))
    operands = (flags, x, top, bot, left, right, *params)
    scratch = [rows_of(8 * tall), rows_of(rows + 8, SIDE)]
    side = tick_call(side_kernel, operands, (8 * tall, chan), tall, SIDE, scratch)
    got_side = onward(side)
    blocks = keep_call(main, side, x.shape)
    operands = (flags, got_main, fresh, top, bot, *params)
    scratch = [rows_of(tall, cols)]
    shape = (rows * cols, chan)
    middle = tick_call(late_main_kernel, operands, shape, rows, cols, scratch)
    operands = (flags, got_main, got_side, middle, fresh, top, bot, left, right, *params, blocks)
    scratch = [
        rows_of(tall, SIDE),
        rows_of(rows, cols),
        pltpu.VMEM((rows * cols, chan), BF16),
        pltpu.SemaphoreType.DMA((rows,)),
    ]
    blocks = tick_call(late_side_kernel, operands, blocks.shape, rows, SIDE, scratch, last=True)
    return blocks.reshape(2, 1, rows, cols, chan)


def solution(mesh):
    in_specs = (
        P("section", "row", "col", None),
        P("row", "col", None),
        P("section", None, None, None, None),
        P("section", None, None, None, None),
        P("section", None, None),
        P("section", None, None),
    )
    out_specs = P(None, "section", "row", "col", None)
    return jax.shard_map(
        per_device, mesh=mesh, in_specs=in_specs, out_specs=out_specs, check_vma=False
    )
```

profile of v0, /device:TPU:185, one launch (start us, length us, event | category | flops | bytes accessed | tf_op | source)
XLA Modules:
  0.0 54.3 jit_solution(14780468514609693040)
XLA Ops:
  0.0 0.9 %edge.1 = (bf16[6,32,256]{2,1,0:T(8,128)(2,1)S(1)}, bf16[6,32,256]{2,1,0:T(8,128)(2,1)S(1)}) custom-call(bf16[32,32,256]{2,1,0:T(8,128)(2,1)} %bitcast.13, bf16[32,32,256]{2,1,0:T(8,128)(2,1)} %fresh.5), custom_call_target="tpu_custom_call" | custom-call | tf_op jit(solution)/shard_map/edge/pallas_call | solution.py:309
  0.9 4.6 %collective-permute-start = (bf16[6,32,256]{2,1,0:T(8,128)(2,1)S(1)}, bf16[6,32,256]{2,1,0:T(8,128)(2,1)S(1)}, u32[]{:S(2)}, u32[]{:S(2)}) collective-permute-start(bf16[6,32,256]{2,1,0:T(8,128)(2,1)S(1)} %get-tuple-element.18), channel_id=1, source_target_pairs={{0,32},{32,64},{64,96},{1,33},{33,65},{65,97},{2,34},{34,66},{66,9... | collective-permute-start | bytes 294920 | tf_op jit(solution)/shard_map/ppermute | solution.py:398
  5.5 1.9 %collective-permute-start.1 = (bf16[6,32,256]{2,1,0:T(8,128)(2,1)S(1)}, bf16[6,32,256]{2,1,0:T(8,128)(2,1)S(1)}, u32[]{:S(2)}, u32[]{:S(2)}) collective-permute-start(bf16[6,32,256]{2,1,0:T(8,128)(2,1)S(1)} %get-tuple-element.19), channel_id=1, source_target_pairs={{32,0},{64,32},{96,64},{33,1},{65,33},{97,65},{34,2},{66,34},{98,6... | collective-permute-start | bytes 294920 | tf_op jit(solution)/shard_map/ppermute | solution.py:397
  7.4 0.1 stack.23
  7.6 2.0 %load.1 = (bf16[32,8,256]{2,1,0:T(8,128)(2,1)S(1)}, bf16[32,8,256]{2,1,0:T(8,128)(2,1)S(1)}, bf16[32,32,256]{2,1,0:T(8,128)(2,1)S(1)}, f32[2,256]{1,0:T(2,128)S(...) custom-call(bf16[32,32,256]{2,1,0:T(8,128)(2,1)} %fresh.5, ...), custom_call_target="tpu_custom_call" | custom-call | flops 1073741824 | bytes 4194304 | tf_op jit(solution)/shard_map/load/pallas_call | solution.py:324
  9.6 0.0 collective-permute-done.top
  9.6 1.8 %collective-permute-done.1.bot = bf16[6,32,256]{2,1,0:T(8,128)(2,1)S(1)} collective-permute-done((bf16[6,32,256]{2,1,0:T(8,128)(2,1)S(1)}, bf16[6,32,256]{2,1,0:T(8,128)(2,1)S(1)}, u32[]{:S(2)}, u32[]{:S(2)}) %collective-permute-start.1) | collective-permute-done | bytes 98336 | tf_op jit(solution)/shard_map/ppermute | solution.py:397
  11.4 4.4 %shard_map.64.main = bf16[1008,256]{1,0:T(8,128)(2,1)S(1)} custom-call(s32[5]{0:T(128)S(1)} %convert_element_type.3.flags, bf16[32,32,256]{2,1,0:T(8,128)(2,1)S(1)} %get-tuple-element.17.x, bf16[6,32,256]{2,1,0:T(8,128)(2,1)S(1)} %collective-permute-done.top, bf16[6,32,256]{2,1,0:T(8,128)(2,1)S(1)} %collective-permute-done.1.bot, ...), custom_call_target="tpu_custom_call" | custom-call | flops 2717908992 | bytes 3145728 | tf_op jit(solution)/shard_map/pallas_call | solution.py:295
  15.9 6.1 %collective-permute-start.2 = (bf16[1008,256]{1,0:T(8,128)(2,1)S(1)}, bf16[1008,256]{1,0:T(8,128)(2,1)S(1)}, u32[]{:S(2)}, u32[]{:S(2)}) collective-permute-start(bf16[1008,256]{1,0:T(8,128)(2,1)S(1)} %shard_map.64.main), channel_id=1, source_target_pairs={{0,128},{128,256},{256,384},{1,129},{129,257},{257,385},{2,130},{1... | collective-permute-start | bytes 1548296 | tf_op jit(solution)/shard_map/ppermute | solution.py:411
  22.0 0.1 pack.1
  22.1 3.1 %collective-permute-start.3 = (bf16[232,256]{1,0:T(8,128)(2,1)S(1)}, bf16[232,256]{1,0:T(8,128)(2,1)S(1)}, u32[]{:S(2)}, u32[]{:S(2)}) collective-permute-start(bf16[232,256]{1,0:T(8,128)(2,1)S(1)} %get-tuple-element.27), channel_id=1, source_target_pairs={{0,1},{1,2},{2,3},{3,4},{4,5},{5,6},{6,7},{7,8},{8,9},{9,10},{10,1... | collective-permute-start | bytes 356360 | tf_op jit(solution)/shard_map/ppermute | solution.py:415
  25.2 4.3 %collective-permute-start.4 = (bf16[232,256]{1,0:T(8,128)(2,1)S(1)}, bf16[232,256]{1,0:T(8,128)(2,1)S(1)}, u32[]{:S(2)}, u32[]{:S(2)}) collective-permute-start(bf16[232,256]{1,0:T(8,128)(2,1)S(1)} %get-tuple-element.28), channel_id=1, source_target_pairs={{1,0},{2,1},{3,2},{4,3},{5,4},{6,5},{7,6},{8,7},{9,8},{10,9},{11,1... | collective-permute-start | bytes 356360 | tf_op jit(solution)/shard_map/ppermute | solution.py:416
  29.5 0.3 collective-permute-done.3.left
  29.8 1.5 %collective-permute-done.4.right = bf16[232,256]{1,0:T(8,128)(2,1)S(1)} collective-permute-done((bf16[232,256]{1,0:T(8,128)(2,1)S(1)}, bf16[232,256]{1,0:T(8,128)(2,1)S(1)}, u32[]{:S(2)}, u32[]{:S(2)}) %collective-permute-start.4) | collective-permute-done | bytes 118816 | tf_op jit(solution)/shard_map/ppermute | solution.py:416
  31.3 2.9 %shard_map.65.sides = bf16[288,256]{1,0:T(8,128)(2,1)S(1)} custom-call(s32[5]{0:T(128)S(1)} %convert_element_type.3.flags, bf16[32,32,256]{2,1,0:T(8,128)(2,1)S(1)} %get-tuple-element.17.x, bf16[6,32,256]{2,1,0:T(8,128)(2,1)S(1)} %collective-permute-done.top, bf16[6,32,256]{2,1,0:T(8,128)(2,1)S(1)} %collective-permute-done.1.bot, ...), custom_call_target="tpu_custom_call" | custom-call | flops 1358954496 | bytes 3145728 | tf_op jit(solution)/shard_map/pallas_call | solution.py:295
  34.2 0.0 copy-start
  34.2 4.1 %collective-permute-start.5 = (bf16[288,256]{1,0:T(8,128)(2,1)S(1)}, bf16[288,256]{1,0:T(8,128)(2,1)S(1)}, u32[]{:S(2)}, u32[]{:S(2)}) collective-permute-start(bf16[288,256]{1,0:T(8,128)(2,1)S(1)} %shard_map.65.sides), channel_id=1, source_target_pairs={{0,128},{128,256},{256,384},{1,129},{129,257},{257,385},{2,130},{1... | collective-permute-start | bytes 442376 | tf_op jit(solution)/shard_map/ppermute | solution.py:411
  38.4 1.0 %keep.1._ = bf16[2048,256]{1,0:T(8,128)(2,1)} custom-call(bf16[1008,256]{1,0:T(8,128)(2,1)S(1)} %shard_map.64.main, bf16[288,256]{1,0:T(8,128)(2,1)S(1)} %shard_map.65.sides), custom_call_target="tpu_custom_call" | custom-call | tf_op jit(solution)/shard_map/keep/pallas_call | solution.py:352
  39.4 7.0 %collective-permute-done.2.main = bf16[1008,256]{1,0:T(8,128)(2,1)S(1)} collective-permute-done((bf16[1008,256]{1,0:T(8,128)(2,1)S(1)}, bf16[1008,256]{1,0:T(8,128)(2,1)S(1)}, u32[]{:S(2)}, u32[]{:S(2)}) %collective-permute-start.2) | collective-permute-done | bytes 516128 | tf_op jit(solution)/shard_map/ppermute | solution.py:411
  46.4 0.0 copy-done
  46.4 4.1 %shard_map.66.middle = bf16[1024,256]{1,0:T(8,128)(2,1)S(1)} custom-call(s32[5]{0:T(128)S(1)} %convert_element_type.3.flags, bf16[1008,256]{1,0:T(8,128)(2,1)S(1)} %collective-permute-done.2.main, bf16[32,32,256]{2,1,0:T(8,128)(2,1)S(1)} %copy-done, bf16[6,32,256]{2,1,0:T(8,128)(2,1)S(1)} %collective-permute-done.top, ...), custom_call_target="tpu_custom_call" | custom-call | flops 2415919104 | bytes 3145728 | tf_op jit(solution)/shard_map/pallas_call | solution.py:295
  50.5 0.0 collective-permute-done.5.sides
  50.5 3.8 %shard_map.67 = bf16[2048,256]{1,0:T(8,128)(2,1)} custom-call(s32[5]{0:T(128)S(1)} %convert_element_type.3.flags, bf16[1008,256]{1,0:T(8,128)(2,1)S(1)} %collective-permute-done.2.main, bf16[288,256]{1,0:T(8,128)(2,1)S(1)} %collective-permute-done.5.sides, bf16[1024,256]{1,0:T(8,128)(2,1)S(1)} %shard_map.66.middle, ...), custom_call_target="tpu_custom_call", output_to_operand_aliasing={{}: (13, {})} | custom-call | flops 1207959552 | bytes 3145728 | tf_op jit(solution)/shard_map/pallas_call | solution.py:295
  (1 shorter events, 0.0 us)
Async XLA Ops:
  0.9 8.7 %collective-permute-start = (bf16[6,32,256]{2,1,0:T(8,128)(2,1)S(1)}, bf16[6,32,256]{2,1,0:T(8,128)(2,1)S(1)}, u32[]{:S(2)}, u32[]{:S(2)}) collective-permute-start(bf16[6,32,256]{2,1,0:T(8,128)(2,1)S(1)} %get-tuple-element.18), channel_id=1, source_target_pairs={{0,32},{32,64},{64,96},{1,33},{33,65},{65,97},{2,34},{34,66},{66,9... | collective-permute-start | bytes 294920 | tf_op jit(solution)/shard_map/ppermute | solution.py:398
  5.5 5.9 %collective-permute-start.1 = (bf16[6,32,256]{2,1,0:T(8,128)(2,1)S(1)}, bf16[6,32,256]{2,1,0:T(8,128)(2,1)S(1)}, u32[]{:S(2)}, u32[]{:S(2)}) collective-permute-start(bf16[6,32,256]{2,1,0:T(8,128)(2,1)S(1)} %get-tuple-element.19), channel_id=1, source_target_pairs={{32,0},{64,32},{96,64},{33,1},{65,33},{97,65},{34,2},{66,34},{98,6... | collective-permute-start | bytes 294920 | tf_op jit(solution)/shard_map/ppermute | solution.py:397
  15.9 30.6 %collective-permute-start.2 = (bf16[1008,256]{1,0:T(8,128)(2,1)S(1)}, bf16[1008,256]{1,0:T(8,128)(2,1)S(1)}, u32[]{:S(2)}, u32[]{:S(2)}) collective-permute-start(bf16[1008,256]{1,0:T(8,128)(2,1)S(1)} %shard_map.64.main), channel_id=1, source_target_pairs={{0,128},{128,256},{256,384},{1,129},{129,257},{257,385},{2,130},{1... | collective-permute-start | bytes 1548296 | tf_op jit(solution)/shard_map/ppermute | solution.py:411
  22.1 7.7 %collective-permute-start.3 = (bf16[232,256]{1,0:T(8,128)(2,1)S(1)}, bf16[232,256]{1,0:T(8,128)(2,1)S(1)}, u32[]{:S(2)}, u32[]{:S(2)}) collective-permute-start(bf16[232,256]{1,0:T(8,128)(2,1)S(1)} %get-tuple-element.27), channel_id=1, source_target_pairs={{0,1},{1,2},{2,3},{3,4},{4,5},{5,6},{6,7},{7,8},{8,9},{9,10},{10,1... | collective-permute-start | bytes 356360 | tf_op jit(solution)/shard_map/ppermute | solution.py:415
  25.2 6.1 %collective-permute-start.4 = (bf16[232,256]{1,0:T(8,128)(2,1)S(1)}, bf16[232,256]{1,0:T(8,128)(2,1)S(1)}, u32[]{:S(2)}, u32[]{:S(2)}) collective-permute-start(bf16[232,256]{1,0:T(8,128)(2,1)S(1)} %get-tuple-element.28), channel_id=1, source_target_pairs={{1,0},{2,1},{3,2},{4,3},{5,4},{6,5},{7,6},{8,7},{9,8},{10,9},{11,1... | collective-permute-start | bytes 356360 | tf_op jit(solution)/shard_map/ppermute | solution.py:416
  34.2 12.2 %copy-start = (bf16[32,32,256]{2,1,0:T(8,128)(2,1)S(1)}, bf16[32,32,256]{2,1,0:T(8,128)(2,1)}, u32[]{:S(2)}) copy-start(bf16[32,32,256]{2,1,0:T(8,128)(2,1)} %fresh.5) | copy-start | bytes 1572868
  34.2 16.3 %collective-permute-start.5 = (bf16[288,256]{1,0:T(8,128)(2,1)S(1)}, bf16[288,256]{1,0:T(8,128)(2,1)S(1)}, u32[]{:S(2)}, u32[]{:S(2)}) collective-permute-start(bf16[288,256]{1,0:T(8,128)(2,1)S(1)} %shard_map.65.sides), channel_id=1, source_target_pairs={{0,128},{128,256},{256,384},{1,129},{129,257},{257,385},{2,130},{1... | collective-permute-start | bytes 442376 | tf_op jit(solution)/shard_map/ppermute | solution.py:411
where the time goes:
time: 54.6 us; the launch traced here: 54.3 us
  starting transfers between devices  24.1 us (44%)
  Pallas kernels  19.2 us (35%)
  waiting for transfers between devices  10.7 us (20%)
    pallas_call x4, Pallas kernels, tick_call(): pl.pallas_call(body, out_shape=jax.ShapeDtypeStruct(out_shape, BF16), in_...  15.1 us
    ppermute x2, starting transfers between devices, onward(): return lax.ppermute(message, 'section', moves('section', 1))  10.3 us
    ppermute x2, waiting for transfers between devices, onward(): return lax.ppermute(message, 'section', moves('section', 1))  7.04 us
    ppermute x1, starting transfers between devices, per_device(): top = lax.ppermute(down, 'row', moves('row', 1))  4.56 us
    ppermute x1, starting transfers between devices, per_device(): right = lax.ppermute(to_left, 'col', moves('col', -1))  4.27 us
    ppermute x1, starting transfers between devices, per_device(): left = lax.ppermute(to_right, 'col', moves('col', 1))  3.12 us
    pallas_call x1, Pallas kernels, load_call(): pl.pallas_call(load_kernel, out_shape=[jax.ShapeDtypeStruct(shape, kind)...  2.02 us
    ppermute x1, starting transfers between devices, per_device(): bot = lax.ppermute(up, 'row', moves('row', -1))  1.92 us
  transfers between devices with their start and end apart: 6, of which 4 were waited for; matrix products, arithmetic and copies ran while one was open for 0% of the time, Pallas kernels for 19%

commit v1 on v0

--- a/solution.py
+++ b/solution.py
@@ -183,13 +183,15 @@
         row[n, 0:2] = edge[2:4]
         row[n, 2 : cols - 2] = main[inner * p : inner * (p + 1)].astype(F32)
         row[n, cols - 2 : cols] = edge[4:6]
-        osc[n * cols : (n + 1) * cols] = row[n].astype(BF16)
-    copy = pltpu.make_async_copy(osc, blocks.at[pl.ds(0, rows * cols)], sem)
+        osc[n] = row[n].astype(BF16)
+    copy = pltpu.make_async_copy(osc, blocks.at[pl.ds(0, rows)], sem)
     copy.start()
     copy.wait()
 
 
-def late_main_kernel(flags, main, fresh, top, bot, gains, shifts, k1, k2, out, x3, h3, row):
+def late_main_kernel(
+    flags, main, fresh, top, bot, gains, shifts, k1, k2, _, blocks, strips, x3, h3, row, out, sems
+):
     rows, cols, chan = fresh.shape
     inner = cols - 4
 
@@ -208,16 +210,28 @@
     for p in range(rows + 4):
         stack_row(x3, p, row[p])
 
+    copies = []
+
     def emit(i, values):
         for r, value in enumerate(values):
-            out[(i + r) * cols : (i + r + 1) * cols] = value.astype(BF16)
+            out[i + r] = value.astype(BF16)
+            strips[0, i + r] = value[0:8]
+            strips[1, i + r] = value[cols - 8 : cols]
+        size = len(values)
+        copy = pltpu.make_async_copy(
+            out.at[pl.ds(i, size)], blocks.at[pl.ds(rows + i, size)], sems.at[len(copies)]
+        )
+        copy.start()
+        copies.append(copy)
 
     weights = gains, shifts, k1, k2
     convolutions(flags, rows, cols, 0, 0, rows, x3, h3, weights, emit)
+    for copy in copies:
+        copy.wait()
 
 
 def late_side_kernel(
-    flags, main, sides, middle, fresh, top, bot, left, right, gains, shifts, k1, k2, _, blocks, x3, h3, row,
+    flags, main, sides, strips, fresh, top, bot, left, right, gains, shifts, k1, k2, _, blocks, x3, h3, row,
     full, osc, sems
 ):
     rows, cols, _ = fresh.shape
@@ -250,19 +264,21 @@
     def emit(i, values):
         for r, value in enumerate(values):
             n = i + r
-            here = slice(n * cols, (n + 1) * cols)
-            full[n] = middle[here].astype(F32)
-            full[n, 0:4] = value[2:6]
-            full[n, cols - 4 : cols] = value[10:14]
-            osc[here] = full[n].astype(BF16)
-        size = len(values) * cols
-        copy = pltpu.make_async_copy(
-            osc.at[pl.ds(i * cols, size)],
-            blocks.at[pl.ds((rows + i) * cols, size)],
-            sems.at[len(copies)],
-        )
-        copy.start()
-        copies.append(copy)
+            full[0, n] = strips[0, n]
+            full[0, n, 0:4] = value[2:6]
+            full[1, n] = strips[1, n]
+            full[1, n, 4:8] = value[10:14]
+            osc[0, n] = full[0, n].astype(BF16)
+            osc[1, n] = full[1, n].astype(BF16)
+        size = len(values)
+        for side, at in enumerate((0, cols - 8)):
+            copy = pltpu.make_async_copy(
+                osc.at[side, pl.ds(i, size)],
+                blocks.at[pl.ds(rows + i, size), pl.ds(at, 8)],
+                sems.at[len(copies)],
+            )
+            copy.start()
+            copies.append(copy)
 
     weights = gains, shifts, k1, k2
     convolutions(flags, rows, SIDE, 2, 0, rows, x3, h3, weights, emit)
@@ -283,22 +299,24 @@
     )
 
 
-def tick_call(body, operands, out_shape, count, pitch, scratch, last=False):
-    chan = out_shape[1]
+def tick_call(body, operands, out_shape, count, pitch, scratch, block=False, strips=()):
+    chan = out_shape[-1]
     stacks = [
         pltpu.VMEM(((count + 4) * pitch, 3 * chan), BF16),
         pltpu.VMEM(((count + 2) * pitch, 3 * chan), BF16),
     ]
     spaces = [SMEM] + [VM] * (len(operands) - 1)
-    if last:
+    if block:
         spaces[-1] = HBM
+    shapes = [jax.ShapeDtypeStruct(out_shape, BF16), *(jax.ShapeDtypeStruct(s, F32) for s in strips)]
+    targets = [HBM if block else VM] + [VM] * len(strips)
     return pl.pallas_call(
         body,
-        out_shape=jax.ShapeDtypeStruct(out_shape, BF16),
+        out_shape=shapes if strips else shapes[0],
         in_specs=spaces,
-        out_specs=HBM if last else VM,
+        out_specs=targets if strips else targets[0],
         scratch_shapes=stacks + scratch,
-        input_output_aliases={len(operands) - 1: 0} if last else {},
+        input_output_aliases={len(operands) - 1: 0} if block else {},
         compiler_params=pltpu.CompilerParams(**PARAMS),
         cost_estimate=cost(count, pitch, chan),
     )(*operands)
@@ -351,12 +369,12 @@
     rows, cols, chan = shape
     return pl.pallas_call(
         functools.partial(keep_kernel, rows=rows, cols=cols),
-        out_shape=jax.ShapeDtypeStruct((2 * rows * cols, chan), BF16),
+        out_shape=jax.ShapeDtypeStruct((2 * rows, cols, chan), BF16),
         in_specs=[VM, VM],
         out_specs=HBM,
         scratch_shapes=[
-            pltpu.VMEM((rows * cols, chan), BF16),
-            pltpu.VMEM((rows, cols, chan), F32),
+            pltpu.VMEM(shape, BF16),
+            pltpu.VMEM(shape, F32),
             pltpu.SemaphoreType.DMA,
         ],
         compiler_params=pltpu.CompilerParams(**PARAMS),
@@ -419,18 +437,23 @@
     side = tick_call(side_kernel, operands, (8 * tall, chan), tall, SIDE, scratch)
     got_side = onward(side)
     blocks = keep_call(main, side, x.shape)
-    operands = (flags, got_main, fresh, top, bot, *params)
-    scratch = [rows_of(tall, cols)]
-    shape = (rows * cols, chan)
-    middle = tick_call(late_main_kernel, operands, shape, rows, cols, scratch)
-    operands = (flags, got_main, got_side, middle, fresh, top, bot, left, right, *params, blocks)
+    operands = (flags, got_main, fresh, top, bot, *params, blocks)
+    scratch = [
+        rows_of(tall, cols),
+        pltpu.VMEM(x.shape, BF16),
+        pltpu.SemaphoreType.DMA((rows,)),
+    ]
+    blocks, strips = tick_call(
+        late_main_kernel, operands, blocks.shape, rows, cols, scratch, block=True, strips=((2, rows, 8, chan),)
+    )
+    operands = (flags, got_main, got_side, strips, fresh, top, bot, left, right, *params, blocks)
     scratch = [
         rows_of(tall, SIDE),
-        rows_of(rows, cols),
-        pltpu.VMEM((rows * cols, chan), BF16),
+        rows_of(2, rows, 8),
+        pltpu.VMEM((2, rows, 8, chan), BF16),
         pltpu.SemaphoreType.DMA((rows,)),
     ]
-    blocks = tick_call(late_side_kernel, operands, blocks.shape, rows, SIDE, scratch, last=True)
+    blocks = tick_call(late_side_kernel, operands, blocks.shape, rows, SIDE, scratch, block=True)
     return blocks.reshape(2, 1, rows, cols, chan)
 
 

time: 54.6 us -> 55.6 us (1.018)
  Pallas kernels: 19.2 us -> 20.2 us
    pallas_call x4, Pallas kernels: 15.1 us -> 16.1 us  [tick_call(): pl.pallas_call(body, out_shape=shapes if strips else shapes[0], in_specs=...]
  transfers between devices with their start and end apart: 6 -> 6, of which waited for: 4 -> 4; matrix products, arithmetic and copies ran while one was open for 0% -> 0% of each run, Pallas kernels for 19% -> 20%
where the time goes in v1:
time: 55.6 us; the launch traced here: 55.3 us
  starting transfers between devices  24.1 us (43%)
  Pallas kernels  20.2 us (36%)
  waiting for transfers between devices  10.7 us (19%)
    pallas_call x4, Pallas kernels, tick_call(): pl.pallas_call(body, out_shape=shapes if strips else shapes[0], in_specs=...  16.1 us
    ppermute x2, starting transfers between devices, onward(): return lax.ppermute(message, 'section', moves('section', 1))  10.3 us
    ppermute x2, waiting for transfers between devices, onward(): return lax.ppermute(message, 'section', moves('section', 1))  7.04 us
    ppermute x1, starting transfers between devices, per_device(): top = lax.ppermute(down, 'row', moves('row', 1))  4.56 us
    ppermute x1, starting transfers between devices, per_device(): right = lax.ppermute(to_left, 'col', moves('col', -1))  4.27 us
    ppermute x1, starting transfers between devices, per_device(): left = lax.ppermute(to_right, 'col', moves('col', 1))  3.12 us
    pallas_call x1, Pallas kernels, load_call(): pl.pallas_call(load_kernel, out_shape=[jax.ShapeDtypeStruct(shape, kind)...  2.02 us
    ppermute x1, starting transfers between devices, per_device(): bot = lax.ppermute(up, 'row', moves('row', -1))  1.92 us
  transfers between devices with their start and end apart: 6, of which 4 were waited for; matrix products, arithmetic and copies ran while one was open for 0% of the time, Pallas kernels for 20%

profile of v1, /device:TPU:185, one launch (start us, length us, event | category | flops | bytes accessed | tf_op | source)
XLA Modules:
  0.0 55.3 jit_solution(8041007921584004329)
XLA Ops:
  0.0 0.9 %edge.1 = (bf16[6,32,256]{2,1,0:T(8,128)(2,1)S(1)}, bf16[6,32,256]{2,1,0:T(8,128)(2,1)S(1)}) custom-call(bf16[32,32,256]{2,1,0:T(8,128)(2,1)} %bitcast.13, bf16[32,32,256]{2,1,0:T(8,128)(2,1)} %fresh.5), custom_call_target="tpu_custom_call" | custom-call | tf_op jit(solution)/shard_map/edge/pallas_call | solution.py:327
  0.9 4.6 %collective-permute-start = (bf16[6,32,256]{2,1,0:T(8,128)(2,1)S(1)}, bf16[6,32,256]{2,1,0:T(8,128)(2,1)S(1)}, u32[]{:S(2)}, u32[]{:S(2)}) collective-permute-start(bf16[6,32,256]{2,1,0:T(8,128)(2,1)S(1)} %get-tuple-element.20), channel_id=1, source_target_pairs={{0,32},{32,64},{64,96},{1,33},{33,65},{65,97},{2,34},{34,66},{66,9... | collective-permute-start | bytes 294920 | tf_op jit(solution)/shard_map/ppermute | solution.py:416
  5.5 1.9 %collective-permute-start.1 = (bf16[6,32,256]{2,1,0:T(8,128)(2,1)S(1)}, bf16[6,32,256]{2,1,0:T(8,128)(2,1)S(1)}, u32[]{:S(2)}, u32[]{:S(2)}) collective-permute-start(bf16[6,32,256]{2,1,0:T(8,128)(2,1)S(1)} %get-tuple-element.21), channel_id=1, source_target_pairs={{32,0},{64,32},{96,64},{33,1},{65,33},{97,65},{34,2},{66,34},{98,6... | collective-permute-start | bytes 294920 | tf_op jit(solution)/shard_map/ppermute | solution.py:415
  7.4 0.1 stack.23
  7.6 2.0 %load.1 = (bf16[32,8,256]{2,1,0:T(8,128)(2,1)S(1)}, bf16[32,8,256]{2,1,0:T(8,128)(2,1)S(1)}, bf16[32,32,256]{2,1,0:T(8,128)(2,1)S(1)}, f32[2,256]{1,0:T(2,128)S(...) custom-call(bf16[32,32,256]{2,1,0:T(8,128)(2,1)} %fresh.5, ...), custom_call_target="tpu_custom_call" | custom-call | flops 1073741824 | bytes 4194304 | tf_op jit(solution)/shard_map/load/pallas_call | solution.py:342
  9.6 0.0 collective-permute-done.top
  9.6 1.8 %collective-permute-done.1.bot = bf16[6,32,256]{2,1,0:T(8,128)(2,1)S(1)} collective-permute-done((bf16[6,32,256]{2,1,0:T(8,128)(2,1)S(1)}, bf16[6,32,256]{2,1,0:T(8,128)(2,1)S(1)}, u32[]{:S(2)}, u32[]{:S(2)}) %collective-permute-start.1) | collective-permute-done | bytes 98336 | tf_op jit(solution)/shard_map/ppermute | solution.py:415
  11.4 4.4 %shard_map.64.main = bf16[1008,256]{1,0:T(8,128)(2,1)S(1)} custom-call(s32[5]{0:T(128)S(1)} %convert_element_type.3.flags, bf16[32,32,256]{2,1,0:T(8,128)(2,1)S(1)} %get-tuple-element.19.x, bf16[6,32,256]{2,1,0:T(8,128)(2,1)S(1)} %collective-permute-done.top, bf16[6,32,256]{2,1,0:T(8,128)(2,1)S(1)} %collective-permute-done.1.bot, ...), custom_call_target="tpu_custom_call" | custom-call | flops 2717908992 | bytes 3145728 | tf_op jit(solution)/shard_map/pallas_call | solution.py:313
  15.9 6.1 %collective-permute-start.2 = (bf16[1008,256]{1,0:T(8,128)(2,1)S(1)}, bf16[1008,256]{1,0:T(8,128)(2,1)S(1)}, u32[]{:S(2)}, u32[]{:S(2)}) collective-permute-start(bf16[1008,256]{1,0:T(8,128)(2,1)S(1)} %shard_map.64.main), channel_id=1, source_target_pairs={{0,128},{128,256},{256,384},{1,129},{129,257},{257,385},{2,130},{1... | collective-permute-start | bytes 1548296 | tf_op jit(solution)/shard_map/ppermute | solution.py:429
  22.0 0.1 pack.1
  22.1 3.1 %collective-permute-start.3 = (bf16[232,256]{1,0:T(8,128)(2,1)S(1)}, bf16[232,256]{1,0:T(8,128)(2,1)S(1)}, u32[]{:S(2)}, u32[]{:S(2)}) collective-permute-start(bf16[232,256]{1,0:T(8,128)(2,1)S(1)} %get-tuple-element.29), channel_id=1, source_target_pairs={{0,1},{1,2},{2,3},{3,4},{4,5},{5,6},{6,7},{7,8},{8,9},{9,10},{10,1... | collective-permute-start | bytes 356360 | tf_op jit(solution)/shard_map/ppermute | solution.py:433
  25.2 4.3 %collective-permute-start.4 = (bf16[232,256]{1,0:T(8,128)(2,1)S(1)}, bf16[232,256]{1,0:T(8,128)(2,1)S(1)}, u32[]{:S(2)}, u32[]{:S(2)}) collective-permute-start(bf16[232,256]{1,0:T(8,128)(2,1)S(1)} %get-tuple-element.30), channel_id=1, source_target_pairs={{1,0},{2,1},{3,2},{4,3},{5,4},{6,5},{7,6},{8,7},{9,8},{10,9},{11,1... | collective-permute-start | bytes 356360 | tf_op jit(solution)/shard_map/ppermute | solution.py:434
  29.5 0.3 collective-permute-done.3.left
  29.8 1.5 %collective-permute-done.4.right = bf16[232,256]{1,0:T(8,128)(2,1)S(1)} collective-permute-done((bf16[232,256]{1,0:T(8,128)(2,1)S(1)}, bf16[232,256]{1,0:T(8,128)(2,1)S(1)}, u32[]{:S(2)}, u32[]{:S(2)}) %collective-permute-start.4) | collective-permute-done | bytes 118816 | tf_op jit(solution)/shard_map/ppermute | solution.py:434
  31.3 2.9 %shard_map.65.sides = bf16[288,256]{1,0:T(8,128)(2,1)S(1)} custom-call(s32[5]{0:T(128)S(1)} %convert_element_type.3.flags, bf16[32,32,256]{2,1,0:T(8,128)(2,1)S(1)} %get-tuple-element.19.x, bf16[6,32,256]{2,1,0:T(8,128)(2,1)S(1)} %collective-permute-done.top, bf16[6,32,256]{2,1,0:T(8,128)(2,1)S(1)} %collective-permute-done.1.bot, ...), custom_call_target="tpu_custom_call" | custom-call | flops 1358954496 | bytes 3145728 | tf_op jit(solution)/shard_map/pallas_call | solution.py:313
  34.2 0.0 copy-start
  34.2 4.1 %collective-permute-start.5 = (bf16[288,256]{1,0:T(8,128)(2,1)S(1)}, bf16[288,256]{1,0:T(8,128)(2,1)S(1)}, u32[]{:S(2)}, u32[]{:S(2)}) collective-permute-start(bf16[288,256]{1,0:T(8,128)(2,1)S(1)} %shard_map.65.sides), channel_id=1, source_target_pairs={{0,128},{128,256},{256,384},{1,129},{129,257},{257,385},{2,130},{1... | collective-permute-start | bytes 442376 | tf_op jit(solution)/shard_map/ppermute | solution.py:429
  38.4 1.0 %keep.1._ = bf16[64,32,256]{2,1,0:T(8,128)(2,1)} custom-call(bf16[1008,256]{1,0:T(8,128)(2,1)S(1)} %shard_map.64.main, bf16[288,256]{1,0:T(8,128)(2,1)S(1)} %shard_map.65.sides), custom_call_target="tpu_custom_call" | custom-call | tf_op jit(solution)/shard_map/keep/pallas_call | solution.py:370
  39.4 7.0 %collective-permute-done.2.main = bf16[1008,256]{1,0:T(8,128)(2,1)S(1)} collective-permute-done((bf16[1008,256]{1,0:T(8,128)(2,1)S(1)}, bf16[1008,256]{1,0:T(8,128)(2,1)S(1)}, u32[]{:S(2)}, u32[]{:S(2)}) %collective-permute-start.2) | collective-permute-done | bytes 516128 | tf_op jit(solution)/shard_map/ppermute | solution.py:429
  46.4 0.0 copy-done
  46.4 5.2 %shard_map.66 = (bf16[64,32,256]{2,1,0:T(8,128)(2,1)}, f32[2,32,8,256]{3,2,1,0:T(8,128)S(1)}) custom-call(s32[5]{0:T(128)S(1)} %convert_element_type.3.flags, bf16[1008,256]{1,0:T(8,128)(2,1)S(1)} %collective-permute-done.2.main, bf16[32,32,256]{2,1,0:T(8,128)(2,1)S(1)} %copy-done, ...), custom_call_target="tpu_custom_call", output_to_operand_aliasing={{0}: (9, {})} | custom-call | flops 2415919104 | bytes 3145728 | tf_op jit(solution)/shard_map/pallas_call | solution.py:313
  51.6 0.0 collective-permute-done.5.sides
  51.6 3.7 %shard_map.67 = bf16[64,32,256]{2,1,0:T(8,128)(2,1)} custom-call(s32[5]{0:T(128)S(1)} %convert_element_type.3.flags, bf16[1008,256]{1,0:T(8,128)(2,1)S(1)} %collective-permute-done.2.main, bf16[288,256]{1,0:T(8,128)(2,1)S(1)} %collective-permute-done.5.sides, f32[2,32,8,256]{3,2,1,0:T(8,128)S(1)} %get-tuple-element.31.strips, ...), custom_call_target="tpu_custom_call", output_to_operand_aliasing={{}: (13, {})} | custom-call | flops 1207959552 | bytes 3145728 | tf_op jit(solution)/shard_map/pallas_call | solution.py:313
  (1 shorter events, 0.0 us)
Async XLA Ops:
  0.9 8.7 %collective-permute-start = (bf16[6,32,256]{2,1,0:T(8,128)(2,1)S(1)}, bf16[6,32,256]{2,1,0:T(8,128)(2,1)S(1)}, u32[]{:S(2)}, u32[]{:S(2)}) collective-permute-start(bf16[6,32,256]{2,1,0:T(8,128)(2,1)S(1)} %get-tuple-element.20), channel_id=1, source_target_pairs={{0,32},{32,64},{64,96},{1,33},{33,65},{65,97},{2,34},{34,66},{66,9... | collective-permute-start | bytes 294920 | tf_op jit(solution)/shard_map/ppermute | solution.py:416
  5.5 5.9 %collective-permute-start.1 = (bf16[6,32,256]{2,1,0:T(8,128)(2,1)S(1)}, bf16[6,32,256]{2,1,0:T(8,128)(2,1)S(1)}, u32[]{:S(2)}, u32[]{:S(2)}) collective-permute-start(bf16[6,32,256]{2,1,0:T(8,128)(2,1)S(1)} %get-tuple-element.21), channel_id=1, source_target_pairs={{32,0},{64,32},{96,64},{33,1},{65,33},{97,65},{34,2},{66,34},{98,6... | collective-permute-start | bytes 294920 | tf_op jit(solution)/shard_map/ppermute | solution.py:415
  15.9 30.6 %collective-permute-start.2 = (bf16[1008,256]{1,0:T(8,128)(2,1)S(1)}, bf16[1008,256]{1,0:T(8,128)(2,1)S(1)}, u32[]{:S(2)}, u32[]{:S(2)}) collective-permute-start(bf16[1008,256]{1,0:T(8,128)(2,1)S(1)} %shard_map.64.main), channel_id=1, source_target_pairs={{0,128},{128,256},{256,384},{1,129},{129,257},{257,385},{2,130},{1... | collective-permute-start | bytes 1548296 | tf_op jit(solution)/shard_map/ppermute | solution.py:429
  22.1 7.7 %collective-permute-start.3 = (bf16[232,256]{1,0:T(8,128)(2,1)S(1)}, bf16[232,256]{1,0:T(8,128)(2,1)S(1)}, u32[]{:S(2)}, u32[]{:S(2)}) collective-permute-start(bf16[232,256]{1,0:T(8,128)(2,1)S(1)} %get-tuple-element.29), channel_id=1, source_target_pairs={{0,1},{1,2},{2,3},{3,4},{4,5},{5,6},{6,7},{7,8},{8,9},{9,10},{10,1... | collective-permute-start | bytes 356360 | tf_op jit(solution)/shard_map/ppermute | solution.py:433
  25.2 6.1 %collective-permute-start.4 = (bf16[232,256]{1,0:T(8,128)(2,1)S(1)}, bf16[232,256]{1,0:T(8,128)(2,1)S(1)}, u32[]{:S(2)}, u32[]{:S(2)}) collective-permute-start(bf16[232,256]{1,0:T(8,128)(2,1)S(1)} %get-tuple-element.30), channel_id=1, source_target_pairs={{1,0},{2,1},{3,2},{4,3},{5,4},{6,5},{7,6},{8,7},{9,8},{10,9},{11,1... | collective-permute-start | bytes 356360 | tf_op jit(solution)/shard_map/ppermute | solution.py:434
  34.2 12.2 %copy-start = (bf16[32,32,256]{2,1,0:T(8,128)(2,1)S(1)}, bf16[32,32,256]{2,1,0:T(8,128)(2,1)}, u32[]{:S(2)}) copy-start(bf16[32,32,256]{2,1,0:T(8,128)(2,1)} %fresh.5) | copy-start | bytes 1572868
  34.2 17.4 %collective-permute-start.5 = (bf16[288,256]{1,0:T(8,128)(2,1)S(1)}, bf16[288,256]{1,0:T(8,128)(2,1)S(1)}, u32[]{:S(2)}, u32[]{:S(2)}) collective-permute-start(bf16[288,256]{1,0:T(8,128)(2,1)S(1)} %shard_map.65.sides), channel_id=1, source_target_pairs={{0,128},{128,256},{256,384},{1,129},{129,257},{257,385},{2,130},{1... | collective-permute-start | bytes 442376 | tf_op jit(solution)/shard_map/ppermute | solution.py:429
